TPU v7x, 32 devices: a 4x4x1 block of a 4x4x8 slice. The times are simulated.
32 devices in a mesh: replica: 1 (over z), data2: 4 (over y), data: 8 (over x, core).
Axes of the slice: x: 4, y: 4, z: 1, core: 2. Of those that a mesh axis runs over, the one named last changes fastest.
The devices are a block of a 4x4x8 slice.
Arguments:
- query_hidden: bfloat16 [128, 32, 2048], P(('replica', 'data2', 'data'))
- doc_hidden: bfloat16 [128, 768, 2048], P(('replica', 'data2', 'data'))
- w_proj: bfloat16 [2048, 128], replicated
- query_mask: int32 [128, 32], P(('replica', 'data2', 'data'))
- doc_mask: int32 [128, 768], P(('replica', 'data2', 'data'))
- temperature: float32 [], replicated
Outputs:
- output 1: float32 [128], P(('replica', 'data2', 'data'))
- output 2: float32 [1], P('replica')
All inputs are finite; a program needn't handle non-finite values.
Results may differ from a plain program's by a relative error of at most 0.001.
Values are sent between devices in bfloat16 or wider.
A program may use at most 768 MiB of HBM per device.

v0:
```python
import jax
import jax.numpy as jnp
from jax import lax
from jax.sharding import PartitionSpec as P


def project_norm(hidden, w_proj):
    projected = jnp.einsum('bld,de->ble', hidden, w_proj, preferred_element_type=jnp.float32)
    norm_len = jnp.sqrt(jnp.sum(projected * projected, axis=-1, keepdims=True))
    return (projected / jnp.maximum(norm_len, 1e-12)).astype(jnp.bfloat16)


def tile_scores(q_block, p_block, doc_valid):
    similarity = jnp.einsum('qtc,jsc->qtjs', q_block, p_block, preferred_element_type=jnp.float32)
    best_match = jnp.max(jnp.where(doc_valid[None, None], similarity, -jnp.inf), axis=-1)
    return jnp.sum(best_match, axis=1)


def solution(mesh):
    outer_size = mesh.shape['data2']
    inner_size = mesh.shape['data']
    group_size = outer_size * inner_size
    batch_axes = ('data2', 'data')
    row_spec = P(('replica', 'data2', 'data'))
    tok_spec = P(('replica', 'data2', 'data'), None, None)
    mask_spec = P(('replica', 'data2', 'data'), None)

    def local_step(query_hidden, doc_hidden, w_proj, query_mask, doc_mask, value_a11):
        local_batch = query_hidden.shape[0]
        total_batch = local_batch * group_size
        q_vecs = project_norm(query_hidden, w_proj)
        q_vecs = jnp.where(query_mask[:, :, None] > 0, q_vecs, jnp.zeros_like(q_vecs))
        p_vecs = project_norm(doc_hidden, w_proj)
        doc_valid = doc_mask > 0
        q_all = lax.all_gather(q_vecs, 'data', axis=0, tiled=True)
        q_all = lax.all_gather(q_all, 'data2', axis=0, tiled=True)
        q_blocks = q_all.reshape(group_size, local_batch, q_all.shape[1], q_all.shape[2])
        column = lax.map(lambda q_block: tile_scores(q_block, p_vecs, doc_valid), q_blocks)
        column = column.reshape(outer_size, inner_size, local_batch, local_batch)
        column = lax.all_to_all(column, 'data', 1, 1, tiled=True)
        column = lax.all_to_all(column, 'data2', 0, 0, tiled=True)
        score_row = jnp.transpose(column, (2, 0, 1, 3)).reshape(local_batch, total_batch)
        logits = score_row / value_a11
        home_index = lax.axis_index('data2') * inner_size + lax.axis_index('data')
        own_logits = lax.dynamic_slice_in_dim(logits, home_index * local_batch, local_batch, axis=1)
        losses = jax.nn.logsumexp(logits, axis=1) - jnp.diagonal(own_logits)
        mean_loss = lax.psum(jnp.sum(losses), batch_axes) / total_batch
        return losses, mean_loss.reshape(1)

    return jax.shard_map(local_step, mesh=mesh, in_specs=(tok_spec, tok_spec, P(None, None), mask_spec, mask_spec, P()), out_specs=(row_spec, P('replica')), check_vma=False)
```

profile of v0, /device:TPU:97, one launch (start us, length us, event | category | flops | bytes accessed | tf_op | source)
XLA Modules:
  0.0 174.5 jit_solution(3524957775136796503)
XLA Ops:
  8.2 1.4 multiply_reduce_fusion.1
  10.4 19.2 %all_gather.6 = bf16[32,32,128]{2,1,0:T(8,128)(2,1)} all-gather(bf16[4,32,128]{2,1,0:T(8,128)(2,1)S(1)} %fusion.8), channel_id=1, replica_groups=mesh['replica'=1,'data2'=4,'data'=8] {'data'}, dimensions={0}, use_global_device_ids=true | all-gather | bytes 294912 | tf_op jit(solution)/shard_map/all_gather | solution.py:35
  29.7 8.9 %multiply_reduce_fusion = (f32[4,768]{1,0:T(4,128)S(1)}, f32[4,768,128]{1,2,0:T(8,128)S(1)}) fusion(bf16[4,768,2048]{2,1,0:T(8,128)(2,1)} %param.9, bf16[2048,128]{1,0:T(8,128)(2,1)S(1)} %copy-done), kind=kOutput, calls=%fused_computation.8 | convolution fusion | flops 1611396096 | bytes 14692352 | tf_op jit(solution)/shard_map/bld,de->ble/dot_general | solution.py:8
  39.3 16.5 %all-gather.2.cloned.1.call-done = bf16[128,32,128]{2,1,0:T(8,128)(2,1)} async-done(((bf16[32,32,128]{2,1,0:T(8,128)(2,1)}), bf16[128,32,128]{2,1,0:T(8,128)(2,1)}) %all-gather.2.cloned.1.call-update) | async-done | bytes 1048592 | tf_op jit(solution)/shard_map/all_gather | solution.py:36
  55.8 42.1 %while.10 = (s32[]{:T(128)}, f32[32,4,4]{2,1,0:T(4,128)S(1)}, pred[4,768]{1,0:T(4,128)(4,1)S(1)}, bf16[32,4,32,128]{3,2,1,0:T(8,128)(2,1)}, bf16[4,768,128]{2,1,0:T(8,128)(2,1)S(1)}, /*index=5*/s32[]{:T(128)}, f32[]{:T(128)}) while((s32[]{:T(128)}, f32[32,4,4]{2,1,0:T(4,128)S(1)}, pred[4,768]{1,0:T(4,128)(4,1)S(1)}, ...), condition=%wide.region_5.6_spmd, body=%wide.region_2.5_spmd.sunk | while | flops 101449712 | bytes 831125 | solution.py:38
  58.4 1.2 select_reduce_fusion.2
  61.1 1.2 select_reduce_fusion.2
  62.4 1.2 select_reduce_fusion.2
  65.0 1.2 select_reduce_fusion.2
  69.0 1.2 select_reduce_fusion.2
  71.6 1.2 select_reduce_fusion.2
  74.2 1.2 select_reduce_fusion.2
  78.2 1.2 select_reduce_fusion.2
  80.8 1.2 select_reduce_fusion.2
  84.8 1.2 select_reduce_fusion.2
  87.4 1.2 select_reduce_fusion.2
  90.0 1.2 select_reduce_fusion.2
  92.7 1.2 select_reduce_fusion.2
  94.0 1.2 select_reduce_fusion.2
  96.6 1.2 select_reduce_fusion.2
  98.0 11.8 %all_to_all.10 = f32[4,8,4,4]{3,0,2,1:T(4,128)S(1)} all-to-all(f32[4,8,4,4]{3,0,2,1:T(4,128)S(1)} %copy.20), channel_id=1, replica_groups=mesh['replica'=1,'data2'=4,'data'=8] {'data'}, dimensions={1} | all-to-all | bytes 4096 | tf_op jit(solution)/shard_map/all_to_all | solution.py:40
  110.7 3.3 %all-to-all-start.1 = ((f32[4,1,128]{2,1,0:T(1,128)}), f32[4,1,128]{2,1,0:T(1,128)S(1)}, u32[]{:S(2)}, u32[]{:S(2)}) async-start(f32[4,1,128]{2,1,0:T(1,128)} %reshape.53), calls=%async_computation.1 | async-start | bytes 4096 | tf_op jit(solution)/shard_map/all_to_all | solution.py:41
  114.7 3.2 %all-to-all-done.1 = f32[4,1,128]{2,1,0:T(1,128)S(1)} async-done(((f32[4,1,128]{2,1,0:T(1,128)}), f32[4,1,128]{2,1,0:T(1,128)S(1)}, u32[]{:S(2)}, u32[]{:S(2)}) %all-to-all-start.1) | async-done | bytes 2080 | tf_op jit(solution)/shard_map/all_to_all | solution.py:41
  121.6 44.3 %psum.7 = f32[]{:T(128)} all-reduce(f32[]{:T(128)} %get-tuple-element.60), channel_id=1, replica_groups=mesh['replica'=1,'data2'=4,'data'=8] {'data2','data'}, use_global_device_ids=true, to_apply=%region_9.10 | all-reduce | flops 1 | bytes 8 | tf_op jit(solution)/shard_map/psum | solution.py:47
  (110 shorter events, 31.0 us)
Async XLA Ops:
  7.2 1.0 copy-start
  7.2 48.6 %all-gather.2.cloned.1.call-start = ((), (), s32[]{:S(2)}) async-start(), calls=%async_computation.2 | async-start | bytes 1310720 | tf_op jit(solution)/shard_map/all_gather | solution.py:36
  38.6 0.7 copy-start.1
  110.7 7.2 %all-to-all-start.1 = ((f32[4,1,128]{2,1,0:T(1,128)}), f32[4,1,128]{2,1,0:T(1,128)S(1)}, u32[]{:S(2)}, u32[]{:S(2)}) async-start(f32[4,1,128]{2,1,0:T(1,128)} %reshape.53), calls=%async_computation.1 | async-start | bytes 4096 | tf_op jit(solution)/shard_map/all_to_all | solution.py:41
Sparse Core Ops, SparseCore 0:
  29.8 25.9 all-gather.1
where the time goes:
time: 177 us; the launch traced here: 175 us
  blocking collectives  75.3 us (43%)
  matrix products  49 us (28%)
  waiting for transfers between devices  19.7 us (11%)
  between operations  16.6 us (9%)
  other arithmetic  5.88 us (3%)
  local copies, waits for them, and re-layouts  4.42 us (2%)
  starting transfers between devices  3.4 us (2%)
    psum x1, blocking collectives, local_step(): mean_loss = lax.psum(jnp.sum(losses), batch_axes) / total_batch  44.3 us
    dot_general x32, matrix products, tile_scores(): jnp.einsum('qtc,jsc->qtjs', q_block, p_block, preferred_element_type=jnp....  38.8 us
    all_gather x1, blocking collectives, local_step(): q_all = lax.all_gather(q_vecs, 'data', axis=0, tiled=True)  19.2 us
    all_gather x1, waiting for transfers between devices, local_step(): q_all = lax.all_gather(q_all, 'data2', axis=0, tiled=True)  16.5 us
    all_to_all x1, blocking collectives, local_step(): column = lax.all_to_all(column, 'data', 1, 1, tiled=True)  11.8 us
    dot_general x2, matrix products, project_norm(): jnp.einsum('bld,de->ble', hidden, w_proj, preferred_element_type=jnp.floa...  10.3 us
  transfers between devices with their start and end apart: 2, of which 2 were waited for; matrix products, arithmetic and copies ran while one was open for 5% of the time, Pallas kernels for 0%

commit v1 on v0

v1 whole, which is shorter than its diff:
```python
import functools

import jax
import jax.numpy as jnp
from jax import lax
from jax.experimental import pallas as pl
from jax.experimental.pallas import tpu as pltpu
from jax.sharding import PartitionSpec as P

MESH = pl.DeviceIdType.MESH
F32 = jnp.float32
BF16 = jnp.bfloat16
CORES = 2


def chip_order(ny, nx):
    def hops(d, n):
        return min(d, n - d)
    return sorted(
        ((dy, dx) for dy in range(ny) for dx in range(nx)),
        key=lambda o: (hops(o[0], ny) + hops(o[1], nx), max(hops(o[0], ny), hops(o[1], nx)), o),
    )


def kernel(cfg, q_hbm, d_hbm, w_hbm, qm_hbm, dm_hbm, temp_hbm, loss_ref, mean_ref,
           qbuf, dbuf, wbuf, qmbuf, dmbuf, dm8, tbuf, qt_all, p_buf, mcol, s_all,
           insem, dsem, qsend, qrecv, fsend, frecv, ssend, srecv):
    ny, nx, nq, qlen, ndoc, dlen, chunk, rows = cfg
    nchip = ny * nx
    ndev = nchip * CORES
    proj = w_hbm.shape[1]
    lanes = nq * qlen
    nchunk = ndoc * dlen // chunk
    per_doc = dlen // chunk
    group = 2
    order = chip_order(ny, nx)

    y = lax.axis_index("data2")
    dx_ = lax.axis_index("data")
    x = dx_ // CORES
    core = dx_ % CORES
    chip = y * nx + x
    me = chip * CORES + core
    other = 1 - core

    def rel(k):
        oy, ox = order[k]
        cy = lax.rem(y + oy, ny)
        cx = lax.rem(x + ox, nx)
        return cy, cx, cy * nx + cx

    def dev(cy, cx, c):
        return {"data2": cy, "data": cx * CORES + c}

    copies = [
        pltpu.make_async_copy(q_hbm, qbuf, insem.at[0]),
        pltpu.make_async_copy(w_hbm, wbuf, insem.at[1]),
        pltpu.make_async_copy(qm_hbm, qmbuf, insem.at[2]),
        pltpu.make_async_copy(dm_hbm, dmbuf, insem.at[3]),
        pltpu.make_async_copy(temp_hbm, tbuf, insem.at[4]),
    ]
    for cp in copies:
        cp.start()

    def doc_copy(c):
        part = pl.ds(c * chunk, chunk)
        return pltpu.make_async_copy(d_hbm.at[part], dbuf.at[part], dsem.at[c])

    for c in range(nchunk):
        doc_copy(c).start()

    barrier = pltpu.get_barrier_semaphore()
    for k in range(nchip):
        cy, cx, _ = rel(k)
        for c in range(CORES):
            tgt = core if c == 0 else other
            if k == 0 and c == 0:
                continue
            pl.semaphore_signal(barrier, inc=1, device_id=dev(cy, cx, tgt), device_id_type=MESH)

    copies[2].wait()
    lane = lax.broadcasted_iota(jnp.int32, (8, lanes), 1)
    sub = lax.broadcasted_iota(jnp.int32, (8, lanes), 0)
    tok_r = lax.broadcasted_iota(jnp.int32, (qlen, lanes), 0)
    tok_l = lax.broadcasted_iota(jnp.int32, (qlen, lanes), 1)
    spread = jnp.where(tok_l // nq == tok_r, 1.0, 0.0).astype(BF16)
    qm = qmbuf[...].astype(F32).astype(BF16)
    qmw = jnp.dot(qm, spread, preferred_element_type=F32)
    qsub = lax.broadcasted_iota(jnp.int32, (nq, lanes), 0)
    qlan = lax.broadcasted_iota(jnp.int32, (nq, lanes), 1)
    qmu = jnp.sum(jnp.where(qlan % nq == qsub, qmw, 0.0), axis=0, keepdims=True)
    pr = lax.broadcasted_iota(jnp.int32, (lanes, lanes), 0)
    pc = lax.broadcasted_iota(jnp.int32, (lanes, lanes), 1)
    perm = jnp.where((pr % qlen) * nq + pr // qlen == pc, qmu, 0.0).astype(BF16)

    def project(block):
        out = jnp.dot(block, wbuf[...], preferred_element_type=F32)
        ss = jnp.sum(out * out, axis=-1, keepdims=True)
        return out * lax.rsqrt(jnp.maximum(ss, 1e-24))

    copies[0].wait()
    copies[1].wait()
    qn = project(qbuf[...]).T.astype(BF16)
    qt = jnp.dot(qn, perm, preferred_element_type=F32).astype(BF16)
    qt_all[me] = qt

    copies[3].wait()
    dm8[...] = jnp.zeros_like(dm8)
    dm8[0:ndoc, :] = dmbuf[...].astype(F32)
    mt = dm8[...].T
    for j in range(ndoc):
        mcol[pl.ds(j * dlen, dlen), :] = jnp.broadcast_to(mt[:, j:j + 1], (dlen, proj)).astype(BF16)

    pl.semaphore_wait(barrier, nchip * CORES - 1)

    def q_send(k):
        cy, cx, cid = rel(k)
        return pltpu.make_async_remote_copy(
            src_ref=qt_all.at[me], dst_ref=qt_all.at[me],
            send_sem=qsend.at[k], recv_sem=qrecv.at[chip],
            device_id=dev(cy, cx, core), device_id_type=MESH)

    def q_recv(k):
        cy, cx, cid = rel(k)
        slot = cid * CORES + core
        return pltpu.make_async_remote_copy(
            src_ref=qt_all.at[slot], dst_ref=qt_all.at[slot],
            send_sem=qsend.at[k], recv_sem=qrecv.at[cid],
            device_id=dev(cy, cx, core), device_id_type=MESH)

    def forward(k):
        _, _, cid = rel(k)
        slot = cid * CORES + core
        return pltpu.make_async_remote_copy(
            src_ref=qt_all.at[slot], dst_ref=qt_all.at[slot],
            send_sem=fsend.at[k], recv_sem=frecv.at[cid],
            device_id=dev(y, x, other), device_id_type=MESH)

    def forwarded(k):
        _, _, cid = rel(k)
        slot = cid * CORES + other
        return pltpu.make_async_remote_copy(
            src_ref=qt_all.at[slot], dst_ref=qt_all.at[slot],
            send_sem=fsend.at[k], recv_sem=frecv.at[cid],
            device_id=dev(y, x, other), device_id_type=MESH)

    forward(0).start()
    for k in range(1, nchip):
        q_send(k).start()

    for j in range(ndoc):
        for c in range(per_doc):
            cc = j * per_doc + c
            doc_copy(cc).wait()
            part = pl.ds(cc * chunk, chunk)
            p_buf[part, :] = project(dbuf[part, :]).astype(BF16)
        row = dm8[j:j + 1, :]
        pos = lax.broadcasted_iota(jnp.int32, (1, dlen), 1).astype(F32)
        first = jnp.min(jnp.where(row > 0, pos, float(dlen)), axis=-1, keepdims=True)
        pick = jnp.where(pos == first, 1.0, 0.0).astype(BF16)
        part = pl.ds(j * dlen, dlen)
        pj = p_buf[part, :]
        fill = jnp.dot(pick, pj, preferred_element_type=F32).astype(BF16)
        m = mcol[part, :]
        p_buf[part, :] = pj * m + fill * (1 - m)

    def arrive(k):
        if k > 0:
            q_recv(k).wait_recv()
            forward(k).start()

    for k in range(group):
        arrive(k)
    s_acc = jnp.zeros((8, lanes), F32)
    for g in range(0, nchip, group):
        for k in range(g + group, min(g + 2 * group, nchip)):
            arrive(k)
        ids = []
        for k in range(g, g + group):
            forwarded(k).wait_recv()
            _, _, cid = rel(k)
            ids += [cid * CORES, cid * CORES + 1]
        rhs = jnp.concatenate([qt_all[i] for i in ids], axis=1)
        width = rhs.shape[1]
        best = jnp.zeros((8, width), F32)
        wsub = lax.broadcasted_iota(jnp.int32, (8, width), 0)
        for j in range(ndoc):
            acc = None
            for c in range(dlen // rows):
                lhs = p_buf[pl.ds(j * dlen + c * rows, rows), :]
                s = jnp.dot(lhs, rhs, preferred_element_type=F32)
                s = jnp.max(s.reshape(rows // 8, 8, width), axis=0)
                acc = s if acc is None else jnp.maximum(acc, s)
            best = jnp.where(wsub == j, jnp.max(acc, axis=0, keepdims=True), best)
        for n, i in enumerate(ids):
            v = best[:, n * lanes:(n + 1) * lanes]
            shift = lanes // 2
            while shift >= nq:
                v = v + pltpu.roll(v, shift, 1)
                shift //= 2
            s_acc = jnp.where(lane // nq == i, v, s_acc)

    s_all[me] = s_acc[:ndoc, :]

    def s_send(k, c):
        cy, cx, cid = rel(k)
        return pltpu.make_async_remote_copy(
            src_ref=s_all.at[me], dst_ref=s_all.at[me],
            send_sem=ssend.at[k * CORES + c], recv_sem=srecv.at[me],
            device_id=dev(cy, cx, c if k > 0 else other), device_id_type=MESH)

    def s_recv(k, c):
        cy, cx, cid = rel(k)
        c = c if k > 0 else other
        slot = cid * CORES + c
        return pltpu.make_async_remote_copy(
            src_ref=s_all.at[slot], dst_ref=s_all.at[slot],
            send_sem=ssend.at[0], recv_sem=srecv.at[slot],
            device_id=dev(cy, cx, c), device_id_type=MESH)

    peers = [(k, c) for k in range(nchip - 1, 0, -1) for c in range(CORES)] + [(0, 1)]
    for k, c in peers:
        s_send(k, c).start()
    copies[4].wait()
    temp = tbuf[0, 0]
    for k in range(1, nchip):
        q_send(k).wait_send()
    for k in range(nchip):
        forward(k).wait_send()
    for k, c in peers[::-1]:
        s_recv(k, c).wait_recv()

    logits = s_all[...] / temp
    top = jnp.max(jnp.max(logits, axis=0), axis=0, keepdims=True)
    total = jnp.sum(jnp.sum(jnp.exp(logits - top[None]), axis=0), axis=0, keepdims=True)
    dd = lax.broadcasted_iota(jnp.int32, logits.shape, 0)
    dj = lax.broadcasted_iota(jnp.int32, logits.shape, 1)
    dl = lax.broadcasted_iota(jnp.int32, logits.shape, 2)
    own = jnp.where(dd * nq + dj == dl, logits, 0.0)
    diag = jnp.sum(jnp.sum(own, axis=0), axis=0, keepdims=True)
    losses = top + jnp.log(total) - diag
    mean_ref[0] = jnp.sum(losses) / (ndev * nq)
    l1 = lax.broadcasted_iota(jnp.int32, losses.shape, 1)
    for q in range(nq):
        loss_ref[q] = jnp.sum(jnp.where(l1 == me * nq + q, losses, 0.0))

    for k, c in peers:
        s_send(k, c).wait_send()


def solution(mesh):
    ny = mesh.shape["data2"]
    nx = mesh.shape["data"] // CORES
    row_spec = P(("replica", "data2", "data"))
    tok_spec = P(("replica", "data2", "data"), None, None)
    mask_spec = P(("replica", "data2", "data"), None)

    def local_step(query_hidden, doc_hidden, w_proj, query_mask, doc_mask, temperature):
        nq, qlen, hidden = query_hidden.shape
        ndoc, dlen, _ = doc_hidden.shape
        proj = w_proj.shape[1]
        nchip = ny * nx
        ndev = nchip * CORES
        chunk, rows = 256, 128
        cfg = (ny, nx, nq, qlen, ndoc, dlen, chunk, rows)
        nchunk = ndoc * dlen // chunk
        dma = pltpu.SemaphoreType.DMA
        return pl.pallas_call(
            functools.partial(kernel, cfg),
            out_shape=(jax.ShapeDtypeStruct((nq,), F32), jax.ShapeDtypeStruct((1,), F32)),
            in_specs=[pl.BlockSpec(memory_space=pl.ANY)] * 6,
            out_specs=(pl.BlockSpec(memory_space=pltpu.SMEM), pl.BlockSpec(memory_space=pltpu.SMEM)),
            scratch_shapes=[
                pltpu.VMEM((nq * qlen, hidden), BF16),
                pltpu.VMEM((ndoc * dlen, hidden), BF16),
                pltpu.VMEM((hidden, proj), BF16),
                pltpu.VMEM((nq, qlen), jnp.int32),
                pltpu.VMEM((ndoc, dlen), jnp.int32),
                pltpu.VMEM((8, dlen), F32),
                pltpu.SMEM((1, 1), F32),
                pltpu.VMEM((ndev, proj, nq * qlen), BF16),
                pltpu.VMEM((ndoc * dlen, proj), BF16),
                pltpu.VMEM((ndoc * dlen, proj), BF16),
                pltpu.VMEM((ndev, ndoc, ndev * nq), F32),
                dma((5,)), dma((nchunk,)),
                dma((nchip,)), dma((nchip,)), dma((nchip,)), dma((nchip,)),
                dma((ndev,)), dma((ndev,)),
            ],
            compiler_params=pltpu.CompilerParams(
                collective_id=0, has_side_effects=True, vmem_limit_bytes=60 * 1024 * 1024),
        )(query_hidden.reshape(nq * qlen, hidden), doc_hidden.reshape(ndoc * dlen, hidden),
          w_proj, query_mask, doc_mask, temperature.reshape(1, 1))

    return jax.shard_map(local_step, mesh=mesh, in_specs=(tok_spec, tok_spec, P(None, None), mask_spec, mask_spec, P()), out_specs=(row_spec, P("replica")), check_vma=False)
```

time: 177 us -> 40.5 us (0.23); the launches traced: 175 us -> 40.4 us
  blocking collectives: 75.3 us -> 0 us
  matrix products: 49 us -> 0 us
  Pallas kernels: 0 us -> 36.3 us
  waiting for transfers between devices: 19.7 us -> 0 us
  between operations: 16.6 us -> 3.05 us
  other arithmetic: 5.88 us -> 0 us
  starting transfers between devices: 3.4 us -> 0 us
  local copies, waits for them, and re-layouts: 4.42 us -> 1.11 us
    dot_general x34 -> x0, matrix products: 49 us -> none  [the longest x32 38.8 us: tile_scores(): jnp.einsum('qtc,jsc->qtjs', q_block, p_block, preferred_element_type=jnp....]
    psum x1 -> x0, blocking collectives: 44.3 us -> none  [local_step(): mean_loss = lax.psum(jnp.sum(losses), batch_axes) / total_batch]
    pallas_call x0 -> x1, Pallas kernels: none -> 36.3 us  [local_step(): pl.pallas_call(functools.partial(kernel, cfg), out_shape=(jax.ShapeDtypeS...]
    all_gather x1 -> x0, blocking collectives: 19.2 us -> none  [local_step(): q_all = lax.all_gather(q_vecs, 'data', axis=0, tiled=True)]
    all_gather x1 -> x0, waiting for transfers between devices: 16.5 us -> none  [local_step(): q_all = lax.all_gather(q_all, 'data2', axis=0, tiled=True)]
    all_to_all x1 -> x0, blocking collectives: 11.8 us -> none  [local_step(): column = lax.all_to_all(column, 'data', 1, 1, tiled=True)]
    reduce_sum x34 -> x0, other arithmetic: 4.13 us -> none  [the longest x32 2.81 us: tile_scores(): return jnp.sum(best_match, axis=1)]
    all_to_all x1 -> x0, starting transfers between devices: 3.34 us -> none  [local_step(): column = lax.all_to_all(column, 'data2', 0, 0, tiled=True)]
  transfers between devices with their start and end apart: 2 -> 0, of which waited for: 2 -> 0; matrix products, arithmetic and copies ran while one was open for 5% -> 0% of each run, Pallas kernels for 0% -> 0%
where the time goes in v1:
time: 40.5 us; the launch traced here: 40.4 us
  Pallas kernels  36.3 us (90%)
  between operations  3.05 us (8%)
  local copies, waits for them, and re-layouts  1.11 us (3%)
    pallas_call x1, Pallas kernels, local_step(): pl.pallas_call(functools.partial(kernel, cfg), out_shape=(jax.ShapeDtypeS...  36.3 us
    unnamed x1, local copies, waits for them, and re-layouts  1.11 us

profile of v1, /device:TPU:97, one launch (start us, length us, event | category | flops | bytes accessed | tf_op | source)
XLA Modules:
  0.0 40.4 jit_solution(16047415933172906660)
XLA Ops:
  1.3 36.3 %shard_map.77 = (f32[4]{0:T(128)}, f32[1]{0:T(128)}) custom-call(bf16[128,2048]{1,0:T(8,128)(2,1)} %bitcast.5, bf16[3072,2048]{1,0:T(8,128)(2,1)} %bitcast.4, bf16[2048,128]{1,0:T(8,128)(2,1)} %w_hbm.1, s32[4,32]{1,0:T(4,128)} %qm_hbm.1, s32[4,768]{1,0:T(4,128)} %dm_hbm.1, f32[1,1]{1,0:T(1,128)} %bitcast.3.temp_hbm), custom_call_target="tpu_custom_call" | custom-call | tf_op jit(solution)/shard_map/pallas_call | solution.py:268
  37.6 1.1 %copy.11 = f32[4]{0:T(128)} copy(f32[4]{0:T(128)} %get-tuple-element.4) | data formatting | bytes 32

commit v2 on v0

v2 whole, which is shorter than its diff:
```python
import functools

import jax
import jax.numpy as jnp
from jax import lax
from jax.experimental import pallas as pl
from jax.experimental.pallas import tpu as pltpu
from jax.sharding import PartitionSpec as P

MESH = pl.DeviceIdType.MESH
F32 = jnp.float32
BF16 = jnp.bfloat16
CORES = 2


def offsets(n):
    return sorted(range(1, n), key=lambda o: (min(o, n - o), o))


def kernel(cfg, q_hbm, d_hbm, w_hbm, qm_hbm, dm_hbm, temp_hbm, out_ref,
           qbuf, dbuf, wbuf, qmbuf, dmbuf, dm8, tbuf, qt_all, p_buf, mcol, s_all,
           insem, dsem, qrecv, frecv, sems):
    ny, nx, nq, qlen, ndoc, dlen, rows, depth = cfg
    nchip = ny * nx
    ndev = nchip * CORES
    pass_at = 2
    proj = w_hbm.shape[1]
    lanes = nq * qlen
    na, nb = ny, nx
    y = lax.axis_index("data2")
    xc = lax.axis_index("data")
    x = xc // CORES
    core = xc % CORES
    other = 1 - core
    me = (y * nx + x) * CORES + core
    turn = core if ny == nx else 0
    turn_o = other if ny == nx else 0
    a, b = y + turn * (x - y), x + turn * (y - x)
    ao, bo = y + turn_o * (x - y), x + turn_o * (y - x)
    near = [o for o in offsets(na) if min(o, na - o) == 1]
    far = [o for o in offsets(na) if min(o, na - o) > 1]

    def dev(cy, cx, c):
        return {"data2": cy, "data": cx * CORES + c}

    def plane_dev(pa, pb):
        return dev(pa + turn * (pb - pa), pb + turn * (pa - pb), core)

    def step(p, o, n):
        return lax.rem(p + o, n)

    def row_of(c, pa):
        return pl.ds((c * na + pa) * nb, nb)

    def owners(c, t, pa):
        return [((pa + t * (i - pa)) * nx + i + t * (pa - i)) * CORES + c for i in range(nb)]

    def wait_bytes(buf, n, sem):
        pltpu.make_async_copy(buf.at[pl.ds(0, n)], buf.at[pl.ds(0, n)], sem).wait()

    copies = [
        pltpu.make_async_copy(q_hbm, qbuf, insem.at[0]),
        pltpu.make_async_copy(w_hbm, wbuf, insem.at[1]),
        pltpu.make_async_copy(qm_hbm, qmbuf, insem.at[2]),
        pltpu.make_async_copy(dm_hbm, dmbuf, insem.at[3]),
        pltpu.make_async_copy(temp_hbm, tbuf, insem.at[4]),
    ]
    for cp in copies:
        cp.start()

    def doc_copy(j):
        part = pl.ds(j * dlen, dlen)
        return pltpu.make_async_copy(d_hbm.at[part], dbuf.at[part], dsem.at[j])

    for j in range(depth):
        doc_copy(j).start()

    barrier = pltpu.get_barrier_semaphore()
    ring1 = [plane_dev(a, step(b, o, nb)) for o in offsets(nb)[::-1]]
    ring2 = [plane_dev(step(a, o, na), b) for o in offsets(na)]
    partner = dev(y, x, other)
    for d in ring2[::-1] + ring1 + [partner]:
        pl.semaphore_signal(barrier, inc=1, device_id=d, device_id_type=MESH)

    copies[2].wait()
    tok_r = lax.broadcasted_iota(jnp.int32, (qlen, lanes), 0)
    tok_l = lax.broadcasted_iota(jnp.int32, (qlen, lanes), 1)
    spread = jnp.where(tok_l // nq == tok_r, 1.0, 0.0).astype(BF16)
    qm = qmbuf[...].astype(F32).astype(BF16)
    qmw = jnp.dot(qm, spread, preferred_element_type=F32)
    qsub = lax.broadcasted_iota(jnp.int32, (nq, lanes), 0)
    qlan = lax.broadcasted_iota(jnp.int32, (nq, lanes), 1)
    qmu = jnp.sum(jnp.where(qlan % nq == qsub, qmw, 0.0), axis=0, keepdims=True)
    pr = lax.broadcasted_iota(jnp.int32, (lanes, lanes), 0)
    pc = lax.broadcasted_iota(jnp.int32, (lanes, lanes), 1)
    perm = jnp.where((pr % qlen) * nq + pr // qlen == pc, qmu, 0.0).astype(BF16)

    def project(block):
        out = jnp.dot(block, wbuf[...], preferred_element_type=F32)
        ss = jnp.sum(out * out, axis=-1, keepdims=True)
        return out * lax.rsqrt(jnp.maximum(ss, 1e-24))

    copies[0].wait()
    copies[1].wait()
    qn = project(qbuf[...]).T.astype(BF16)
    mine = (core * na + a) * nb + b
    qt_all[mine] = jnp.dot(qn, perm, preferred_element_type=F32).astype(BF16)

    copies[3].wait()
    dm8[...] = jnp.zeros_like(dm8)
    dm8[0:ndoc, :] = dmbuf[...].astype(F32)

    pl.semaphore_wait(barrier, na + nb - 1)

    def send(part, d, send_sem, recv_sem):
        pltpu.make_async_remote_copy(
            src_ref=qt_all.at[part], dst_ref=qt_all.at[part], send_sem=send_sem, recv_sem=recv_sem,
            device_id=d, device_id_type=MESH).start()

    def pass_rows():
        wait_bytes(qt_all, nb - 1, qrecv.at[0])
        for o, d in zip(offsets(na), ring2):
            send(row_of(core, a), d, sems.at[0], qrecv.at[1 if o in near else 2])
        send(row_of(core, a), partner, sems.at[1], frecv.at[0])

    def hand_over(which, steps):
        wait_bytes(qt_all, len(steps) * nb, qrecv.at[which])
        for o in steps:
            send(row_of(core, step(a, o, na)), partner, sems.at[1], frecv.at[which])

    for d in ring1:
        send(pl.ds(mine, 1), d, sems.at[0], qrecv.at[0])

    mt = dm8[...].T

    def fill(j):
        part = pl.ds(j * dlen, dlen)
        row = dm8[j:j + 1, :]
        pos = lax.broadcasted_iota(jnp.int32, (1, dlen), 1).astype(F32)
        first = jnp.min(jnp.where(row > 0, pos, float(dlen)), axis=-1, keepdims=True)
        pick = jnp.where(pos == first, 1.0, 0.0).astype(BF16)
        pj = p_buf[part, :]
        token = jnp.dot(pick, pj, preferred_element_type=F32).astype(BF16)
        m = mcol[part, :]
        p_buf[part, :] = pj * m + token * (1 - m)

    for j in range(ndoc):
        doc_copy(j).wait()
        if j + depth < ndoc:
            doc_copy(j + depth).start()
        if j == pass_at:
            pass_rows()
        for c in range(dlen // rows):
            part = pl.ds(j * dlen + c * rows, rows)
            p_buf[part, :] = project(dbuf[part, :]).astype(BF16)
        mcol[pl.ds(j * dlen, dlen), :] = jnp.broadcast_to(mt[:, j:j + 1], (dlen, proj)).astype(BF16)
        if j > 0:
            fill(j - 1)

    lane = lax.broadcasted_iota(jnp.int32, (8, lanes), 1)
    width = nb * lanes
    wsub = lax.broadcasted_iota(jnp.int32, (8, width), 0)

    def tail(s_acc, best, ids):
        for n, i in enumerate(ids):
            v = best[:, n * lanes:(n + 1) * lanes]
            shift = lanes // 2
            while shift >= nq:
                v = v + pltpu.roll(v, shift, 1)
                shift //= 2
            s_acc = jnp.where(lane // nq == i, v, s_acc)
        return s_acc

    def own(o):
        return core, turn, step(a, o, na)

    def others(o):
        return other, turn_o, step(ao, o, na)

    plan = [(own(0), None), (others(0), lambda: wait_bytes(qt_all, nb, frecv.at[0]))]
    for which, steps in ((1, near), (2, far)):
        todo = [(own(o), None) for o in steps] + [(others(o), None) for o in steps]
        todo[0] = (todo[0][0], functools.partial(hand_over, which, steps))
        todo[len(steps)] = (todo[len(steps)][0], functools.partial(wait_bytes, qt_all, len(steps) * nb, frecv.at[which]))
        plan += todo

    s_acc = jnp.zeros((8, lanes), F32)
    pending = []
    for g, ((c, t, pa), ready) in enumerate(plan):
        if ready is not None:
            ready()
        if g == 0:
            fill(ndoc - 1)
        rhs = qt_all[row_of(c, pa)]
        rhs = jnp.concatenate([rhs[i] for i in range(nb)], axis=1)
        best = jnp.zeros((8, width), F32)
        for j in range(ndoc):
            s = jnp.dot(p_buf[pl.ds(j * dlen, dlen), :], rhs, preferred_element_type=F32)
            s = jnp.max(s.reshape(dlen // 8, 8, width), axis=0)
            best = jnp.where(wsub == j, jnp.max(s, axis=0, keepdims=True), best)
        for item in pending:
            s_acc = tail(s_acc, *item)
        pending = [(best, owners(c, t, pa))]
    for item in pending:
        s_acc = tail(s_acc, *item)
    copies[4].wait()
    s_all[me] = s_acc[:ndoc, :] / tbuf[0]

    peers = [(oy, ox, c) for oy in range(ny) for ox in range(nx) for c in range(CORES)][1:]
    peers.sort(key=lambda p: -min(p[0], ny - p[0]) - min(p[1], nx - p[1]))
    for oy, ox, c in peers:
        pltpu.make_async_remote_copy(
            src_ref=s_all.at[me], dst_ref=s_all.at[me],
            send_sem=sems.at[2], recv_sem=sems.at[3],
            device_id=dev(step(y, oy, ny), step(x, ox, nx), step(core, c, CORES)), device_id_type=MESH).start()
    wait_bytes(qt_all, nb - 1 + (na - 1) * nb, sems.at[0])
    wait_bytes(qt_all, nchip, sems.at[1])
    wait_bytes(s_all, ndev - 1, sems.at[3])

    logits = s_all[...]
    top = jnp.max(jnp.max(logits, axis=0), axis=0, keepdims=True)
    total = jnp.sum(jnp.sum(jnp.exp(logits - top[None]), axis=0), axis=0, keepdims=True)
    dd = lax.broadcasted_iota(jnp.int32, logits.shape, 0)
    dj = lax.broadcasted_iota(jnp.int32, logits.shape, 1)
    dl = lax.broadcasted_iota(jnp.int32, logits.shape, 2)
    diag = jnp.sum(jnp.sum(jnp.where(dd * nq + dj == dl, logits, 0.0), axis=0), axis=0, keepdims=True)
    losses = top + jnp.log(total) - diag
    nrow = ndev * nq
    home = pltpu.roll(jnp.broadcast_to(losses, (8, nrow)), lax.rem(nrow - me * nq, nrow), 1)
    mean = jnp.sum(losses, axis=1, keepdims=True) / nrow
    out_ref[...] = jnp.where(lax.broadcasted_iota(jnp.int32, home.shape, 0) == 0, home, mean)

    wait_bytes(s_all, ndev - 1, sems.at[2])


def finish(vec_ref, loss_ref, mean_ref):
    loss_ref[...] = vec_ref[0, :loss_ref.shape[0]]
    mean_ref[...] = vec_ref[1, :1]


def solution(mesh):
    ny = mesh.shape["data2"]
    nx = mesh.shape["data"] // CORES
    row_spec = P(("replica", "data2", "data"))
    tok_spec = P(("replica", "data2", "data"), None, None)
    mask_spec = P(("replica", "data2", "data"), None)

    def local_step(query_hidden, doc_hidden, w_proj, query_mask, doc_mask, temperature):
        nq, qlen, hidden = query_hidden.shape
        ndoc, dlen, _ = doc_hidden.shape
        proj = w_proj.shape[1]
        ndev = ny * nx * CORES
        rows, depth = 128, 2
        cfg = (ny, nx, nq, qlen, ndoc, dlen, rows, depth)
        dma = pltpu.SemaphoreType.DMA
        vec = pl.pallas_call(
            functools.partial(kernel, cfg),
            out_shape=jax.ShapeDtypeStruct((8, ndev * nq), F32),
            in_specs=[pl.BlockSpec(memory_space=pl.ANY)] * 6,
            out_specs=pl.BlockSpec(memory_space=pltpu.VMEM),
            scratch_shapes=[
                pltpu.VMEM((nq * qlen, hidden), BF16),
                pltpu.VMEM((ndoc * dlen, hidden), BF16),
                pltpu.VMEM((hidden, proj), BF16),
                pltpu.VMEM((nq, qlen), jnp.int32),
                pltpu.VMEM((ndoc, dlen), jnp.int32),
                pltpu.VMEM((8, dlen), F32),
                pltpu.SMEM((1,), F32),
                pltpu.VMEM((ndev, proj, nq * qlen), BF16),
                pltpu.VMEM((ndoc * dlen, proj), BF16),
                pltpu.VMEM((ndoc * dlen, proj), BF16),
                pltpu.VMEM((ndev, ndoc, ndev * nq), F32),
                dma((5,)), dma((ndoc,)), dma((3,)), dma((3,)), dma((4,)),
            ],
            compiler_params=pltpu.CompilerParams(
                collective_id=0, has_side_effects=True, vmem_limit_bytes=60 * 1024 * 1024),
        )(query_hidden.reshape(nq * qlen, hidden), doc_hidden.reshape(ndoc * dlen, hidden),
          w_proj, query_mask, doc_mask, temperature.reshape(1))
        return pl.pallas_call(
            finish,
            out_shape=(jax.ShapeDtypeStruct((nq,), F32), jax.ShapeDtypeStruct((1,), F32)),
            in_specs=[pl.BlockSpec(memory_space=pltpu.VMEM)],
            out_specs=(pl.BlockSpec(memory_space=pltpu.VMEM), pl.BlockSpec(memory_space=pltpu.VMEM)),
        )(vec)

    return jax.shard_map(local_step, mesh=mesh, in_specs=(tok_spec, tok_spec, P(None, None), mask_spec, mask_spec, P()), out_specs=(row_spec, P("replica")), check_vma=False)
```

time: 177 us -> 30.4 us (0.17); the launches traced: 175 us -> 30.2 us
  blocking collectives: 75.3 us -> 0 us
  matrix products: 49 us -> 0 us
  Pallas kernels: 0 us -> 28.9 us
  waiting for transfers between devices: 19.7 us -> 0 us
  between operations: 16.6 us -> 1.29 us
  other arithmetic: 5.88 us -> 0 us
  local copies, waits for them, and re-layouts: 4.42 us -> 0 us
  starting transfers between devices: 3.4 us -> 0 us
    dot_general x34 -> x0, matrix products: 49 us -> none  [the longest x32 38.8 us: tile_scores(): jnp.einsum('qtc,jsc->qtjs', q_block, p_block, preferred_element_type=jnp....]
    psum x1 -> x0, blocking collectives: 44.3 us -> none  [local_step(): mean_loss = lax.psum(jnp.sum(losses), batch_axes) / total_batch]
    pallas_call x0 -> x2, Pallas kernels: none -> 28.9 us  [the longest x1 27.7 us: local_step(): pl.pallas_call(functools.partial(kernel, cfg), out_shape=jax.ShapeDtypeSt...]
    all_gather x1 -> x0, blocking collectives: 19.2 us -> none  [local_step(): q_all = lax.all_gather(q_vecs, 'data', axis=0, tiled=True)]
    all_gather x1 -> x0, waiting for transfers between devices: 16.5 us -> none  [local_step(): q_all = lax.all_gather(q_all, 'data2', axis=0, tiled=True)]
    all_to_all x1 -> x0, blocking collectives: 11.8 us -> none  [local_step(): column = lax.all_to_all(column, 'data', 1, 1, tiled=True)]
    reduce_sum x34 -> x0, other arithmetic: 4.13 us -> none  [the longest x32 2.81 us: tile_scores(): return jnp.sum(best_match, axis=1)]
    all_to_all x1 -> x0, starting transfers between devices: 3.34 us -> none  [local_step(): column = lax.all_to_all(column, 'data2', 0, 0, tiled=True)]
  transfers between devices with their start and end apart: 2 -> 0, of which waited for: 2 -> 0; matrix products, arithmetic and copies ran while one was open for 5% -> 0% of each run, Pallas kernels for 0% -> 0%
where the time goes in v2:
time: 30.4 us; the launch traced here: 30.2 us
  Pallas kernels  28.9 us (95%)
  between operations  1.29 us (4%)
    pallas_call x1, Pallas kernels, local_step(): pl.pallas_call(functools.partial(kernel, cfg), out_shape=jax.ShapeDtypeSt...  27.7 us
    pallas_call x1, Pallas kernels, local_step(): pl.pallas_call(finish, out_shape=(jax.ShapeDtypeStruct((nq,), F32), jax.S...  1.2 us

profile of v2, /device:TPU:97, one launch (start us, length us, event | category | flops | bytes accessed | tf_op | source)
XLA Modules:
  0.0 30.2 jit_solution(9130911447287773948)
XLA Ops:
  1.3 27.7 %shard_map.77.vec_ref = f32[8,128]{1,0:T(8,128)} custom-call(bf16[128,2048]{1,0:T(8,128)(2,1)} %bitcast.5, bf16[3072,2048]{1,0:T(8,128)(2,1)} %bitcast.4, bf16[2048,128]{1,0:T(8,128)(2,1)} %w_hbm.1, s32[4,32]{1,0:T(4,128)} %qm_hbm.1, s32[4,768]{1,0:T(4,128)} %dm_hbm.1, f32[1]{0:T(128)} %bitcast.3.temp_hbm), custom_call_target="tpu_custom_call" | custom-call | tf_op jit(solution)/shard_map/pallas_call | solution.py:256
  29.0 1.2 %shard_map.78 = (f32[4]{0:T(128)}, f32[1]{0:T(128)}) custom-call(f32[8,128]{1,0:T(8,128)} %shard_map.77.vec_ref), custom_call_target="tpu_custom_call" | custom-call | tf_op jit(solution)/shard_map/pallas_call | solution.py:279

commit v3 on v2

--- a/solution.py
+++ b/solution.py
@@ -23,7 +23,8 @@
     ny, nx, nq, qlen, ndoc, dlen, rows, depth = cfg
     nchip = ny * nx
     ndev = nchip * CORES
-    pass_at = 2
+    pass_at = 3
+    wide = 4
     proj = w_hbm.shape[1]
     lanes = nq * qlen
     na, nb = ny, nx
@@ -49,14 +50,20 @@
     def step(p, o, n):
         return lax.rem(p + o, n)
 
-    def row_of(c, pa):
-        return pl.ds((c * na + pa) * nb, nb)
-
-    def owners(c, t, pa):
-        return [((pa + t * (i - pa)) * nx + i + t * (pa - i)) * CORES + c for i in range(nb)]
+    def block(c, i, j):
+        c, t, pa, pb = (core, turn, a, b) if c == 0 else (other, turn_o, ao, bo)
+        pa, pb = step(pa, i, na), step(pb, j, nb)
+        return (c * na + pa) * nb + pb, ((pa + t * (pb - pa)) * nx + pb + t * (pa - pb)) * CORES + c
 
     def wait_bytes(buf, n, sem):
         pltpu.make_async_copy(buf.at[pl.ds(0, n)], buf.at[pl.ds(0, n)], sem).wait()
+
+    barrier = pltpu.get_barrier_semaphore()
+    ring1 = {o: plane_dev(a, step(b, o, nb)) for o in offsets(nb)[::-1]}
+    ring2 = {o: plane_dev(step(a, o, na), b) for o in offsets(na)[::-1]}
+    partner = dev(y, x, other)
+    for d in [*ring2.values(), *ring1.values(), partner]:
+        pl.semaphore_signal(barrier, inc=1, device_id=d, device_id_type=MESH)
 
     copies = [
         pltpu.make_async_copy(q_hbm, qbuf, insem.at[0]),
@@ -74,13 +81,6 @@
 
     for j in range(depth):
         doc_copy(j).start()
-
-    barrier = pltpu.get_barrier_semaphore()
-    ring1 = [plane_dev(a, step(b, o, nb)) for o in offsets(nb)[::-1]]
-    ring2 = [plane_dev(step(a, o, na), b) for o in offsets(na)]
-    partner = dev(y, x, other)
-    for d in ring2[::-1] + ring1 + [partner]:
-        pl.semaphore_signal(barrier, inc=1, device_id=d, device_id_type=MESH)
 
     copies[2].wait()
     tok_r = lax.broadcasted_iota(jnp.int32, (qlen, lanes), 0)
@@ -102,8 +102,10 @@
 
     copies[0].wait()
     copies[1].wait()
+    for j in range(depth, min(depth + 1, ndoc)):
+        doc_copy(j).start()
     qn = project(qbuf[...]).T.astype(BF16)
-    mine = (core * na + a) * nb + b
+    mine = block(0, 0, 0)[0]
     qt_all[mine] = jnp.dot(qn, perm, preferred_element_type=F32).astype(BF16)
 
     copies[3].wait()
@@ -112,25 +114,38 @@
 
     pl.semaphore_wait(barrier, na + nb - 1)
 
-    def send(part, d, send_sem, recv_sem):
+    def send(slot, d, send_sem, recv_sem):
         pltpu.make_async_remote_copy(
-            src_ref=qt_all.at[part], dst_ref=qt_all.at[part], send_sem=send_sem, recv_sem=recv_sem,
+            src_ref=qt_all.at[slot], dst_ref=qt_all.at[slot], send_sem=send_sem, recv_sem=recv_sem,
             device_id=d, device_id_type=MESH).start()
 
-    def pass_rows():
-        wait_bytes(qt_all, nb - 1, qrecv.at[0])
-        for o, d in zip(offsets(na), ring2):
-            send(row_of(core, a), d, sems.at[0], qrecv.at[1 if o in near else 2])
-        send(row_of(core, a), partner, sems.at[1], frecv.at[0])
-
-    def hand_over(which, steps):
-        wait_bytes(qt_all, len(steps) * nb, qrecv.at[which])
-        for o in steps:
-            send(row_of(core, step(a, o, na)), partner, sems.at[1], frecv.at[which])
-
-    for d in ring1:
-        send(pl.ds(mine, 1), d, sems.at[0], qrecv.at[0])
-
+    cross1 = [(0, o) for o in offsets(nb)]
+    cross2 = [(o, 0) for o in offsets(na)]
+    rest = [(i, j) for i in near for j in offsets(nb)] + [(i, j) for i in far for j in offsets(nb)]
+
+    def pass_cross():
+        wait_bytes(qt_all, len(cross1) + len(cross2), qrecv.at[0])
+        wait_bytes(qt_all, 1, frecv.at[0])
+        for i, j in cross1:
+            for o in near:
+                send(block(0, i, j)[0], ring2[o], sems.at[0], qrecv.at[1])
+        for i in far:
+            for o in offsets(nb):
+                send(block(0, i, 0)[0], ring1[o], sems.at[0], qrecv.at[1])
+        for i, j in cross1 + cross2:
+            send(block(0, i, j)[0], partner, sems.at[1], frecv.at[1])
+
+    def pass_rest():
+        wait_bytes(qt_all, len(rest), qrecv.at[1])
+        for i, j in rest:
+            send(block(0, i, j)[0], partner, sems.at[1], frecv.at[2])
+
+    for d in [*ring2.values(), *ring1.values()]:
+        send(mine, d, sems.at[0], qrecv.at[0])
+    send(mine, partner, sems.at[1], frecv.at[0])
+
+    for j in range(depth + 1, ndoc):
+        doc_copy(j).start()
     mt = dm8[...].T
 
     def fill(j):
@@ -146,10 +161,8 @@
 
     for j in range(ndoc):
         doc_copy(j).wait()
-        if j + depth < ndoc:
-            doc_copy(j + depth).start()
         if j == pass_at:
-            pass_rows()
+            pass_cross()
         for c in range(dlen // rows):
             part = pl.ds(j * dlen + c * rows, rows)
             p_buf[part, :] = project(dbuf[part, :]).astype(BF16)
@@ -158,7 +171,7 @@
             fill(j - 1)
 
     lane = lax.broadcasted_iota(jnp.int32, (8, lanes), 1)
-    width = nb * lanes
+    width = wide * lanes
     wsub = lax.broadcasted_iota(jnp.int32, (8, width), 0)
 
     def tail(s_acc, best, ids):
@@ -171,36 +184,33 @@
             s_acc = jnp.where(lane // nq == i, v, s_acc)
         return s_acc
 
-    def own(o):
-        return core, turn, step(a, o, na)
-
-    def others(o):
-        return other, turn_o, step(ao, o, na)
-
-    plan = [(own(0), None), (others(0), lambda: wait_bytes(qt_all, nb, frecv.at[0]))]
-    for which, steps in ((1, near), (2, far)):
-        todo = [(own(o), None) for o in steps] + [(others(o), None) for o in steps]
-        todo[0] = (todo[0][0], functools.partial(hand_over, which, steps))
-        todo[len(steps)] = (todo[len(steps)][0], functools.partial(wait_bytes, qt_all, len(steps) * nb, frecv.at[which]))
-        plan += todo
+    arrivals = [
+        ([(0, 0, 0)] + [(0, *o) for o in cross1] + [(1, 0, 0)] + [(0, *o) for o in cross2], None),
+        ([(1, *o) for o in cross1 + cross2], lambda: wait_bytes(qt_all, len(cross1) + len(cross2), frecv.at[1])),
+        ([(0, *o) for o in rest], pass_rest),
+        ([(1, *o) for o in rest], lambda: wait_bytes(qt_all, len(rest), frecv.at[2])),
+    ]
+    queue = [(where, ready if n == 0 else None) for blocks, ready in arrivals for n, where in enumerate(blocks)]
 
     s_acc = jnp.zeros((8, lanes), F32)
     pending = []
-    for g, ((c, t, pa), ready) in enumerate(plan):
-        if ready is not None:
-            ready()
+    for g in range(0, len(queue), wide):
+        for _, ready in queue[g:g + wide]:
+            if ready is not None:
+                ready()
         if g == 0:
             fill(ndoc - 1)
-        rhs = qt_all[row_of(c, pa)]
-        rhs = jnp.concatenate([rhs[i] for i in range(nb)], axis=1)
+        here = [block(*where) for where, _ in queue[g:g + wide]]
+        rhs = jnp.concatenate([qt_all[slot] for slot, _ in here], axis=1)
         best = jnp.zeros((8, width), F32)
         for j in range(ndoc):
             s = jnp.dot(p_buf[pl.ds(j * dlen, dlen), :], rhs, preferred_element_type=F32)
             s = jnp.max(s.reshape(dlen // 8, 8, width), axis=0)
             best = jnp.where(wsub == j, jnp.max(s, axis=0, keepdims=True), best)
-        for item in pending:
-            s_acc = tail(s_acc, *item)
-        pending = [(best, owners(c, t, pa))]
+            if j == 0:
+                for item in pending:
+                    s_acc = tail(s_acc, *item)
+        pending = [(best, [i for _, i in here])]
     for item in pending:
         s_acc = tail(s_acc, *item)
     copies[4].wait()
@@ -213,7 +223,7 @@
             src_ref=s_all.at[me], dst_ref=s_all.at[me],
             send_sem=sems.at[2], recv_sem=sems.at[3],
             device_id=dev(step(y, oy, ny), step(x, ox, nx), step(core, c, CORES)), device_id_type=MESH).start()
-    wait_bytes(qt_all, nb - 1 + (na - 1) * nb, sems.at[0])
+    wait_bytes(qt_all, nchip - 1, sems.at[0])
     wait_bytes(qt_all, nchip, sems.at[1])
     wait_bytes(s_all, ndev - 1, sems.at[3])
 
@@ -250,12 +260,12 @@
         ndoc, dlen, _ = doc_hidden.shape
         proj = w_proj.shape[1]
         ndev = ny * nx * CORES
-        rows, depth = 128, 2
+        rows, depth = 128, 1
         cfg = (ny, nx, nq, qlen, ndoc, dlen, rows, depth)
         dma = pltpu.SemaphoreType.DMA
         vec = pl.pallas_call(
             functools.partial(kernel, cfg),
-            out_shape=jax.ShapeDtypeStruct((8, ndev * nq), F32),
+            out_shape=pltpu.VMEM((8, ndev * nq), F32),
             in_specs=[pl.BlockSpec(memory_space=pl.ANY)] * 6,
             out_specs=pl.BlockSpec(memory_space=pltpu.VMEM),
             scratch_shapes=[
@@ -270,7 +280,7 @@
                 pltpu.VMEM((ndoc * dlen, proj), BF16),
                 pltpu.VMEM((ndoc * dlen, proj), BF16),
                 pltpu.VMEM((ndev, ndoc, ndev * nq), F32),
-                dma((5,)), dma((ndoc,)), dma((3,)), dma((3,)), dma((4,)),
+                dma((5,)), dma((ndoc,)), dma((2,)), dma((3,)), dma((4,)),
             ],
             compiler_params=pltpu.CompilerParams(
                 collective_id=0, has_side_effects=True, vmem_limit_bytes=60 * 1024 * 1024),
@@ -281,6 +291,7 @@
             out_shape=(jax.ShapeDtypeStruct((nq,), F32), jax.ShapeDtypeStruct((1,), F32)),
             in_specs=[pl.BlockSpec(memory_space=pltpu.VMEM)],
             out_specs=(pl.BlockSpec(memory_space=pltpu.VMEM), pl.BlockSpec(memory_space=pltpu.VMEM)),
+            compiler_params=pltpu.CompilerParams(vmem_limit_bytes=1024 * 1024),
         )(vec)
 
     return jax.shard_map(local_step, mesh=mesh, in_specs=(tok_spec, tok_spec, P(None, None), mask_spec, mask_spec, P()), out_specs=(row_spec, P("replica")), check_vma=False)

time: 30.4 us -> 27.3 us (0.90)
  Pallas kernels: 28.9 us -> 25.9 us
    pallas_call x1, Pallas kernels: 27.7 us -> 25.4 us  [local_step(): pl.pallas_call(functools.partial(kernel, cfg), out_shape=pltpu.VMEM((8, n...]
    pallas_call x1, Pallas kernels: 1.2 us -> 0.52 us  [local_step(): pl.pallas_call(finish, out_shape=(jax.ShapeDtypeStruct((nq,), F32), jax.S...]
where the time goes in v3:
time: 27.3 us; the launch traced here: 27.2 us
  Pallas kernels  25.9 us (95%)
  between operations  1.29 us (5%)
    pallas_call x1, Pallas kernels, local_step(): pl.pallas_call(functools.partial(kernel, cfg), out_shape=pltpu.VMEM((8, n...  25.4 us

profile of v3, /device:TPU:97, one launch (start us, length us, event | category | flops | bytes accessed | tf_op | source)
XLA Modules:
  0.0 27.2 jit_solution(5359152967478739943)
XLA Ops:
  1.3 25.4 %shard_map.77.vec_ref = f32[8,128]{1,0:T(8,128)S(1)} custom-call(bf16[128,2048]{1,0:T(8,128)(2,1)} %bitcast.5, bf16[3072,2048]{1,0:T(8,128)(2,1)} %bitcast.4, bf16[2048,128]{1,0:T(8,128)(2,1)} %w_hbm.1, s32[4,32]{1,0:T(4,128)} %qm_hbm.1, s32[4,768]{1,0:T(4,128)} %dm_hbm.1, f32[1]{0:T(128)} %bitcast.3.temp_hbm), custom_call_target="tpu_custom_call" | custom-call | tf_op jit(solution)/shard_map/pallas_call | solution.py:266
  26.7 0.5 %shard_map.78 = (f32[4]{0:T(128)}, f32[1]{0:T(128)}) custom-call(f32[8,128]{1,0:T(8,128)S(1)} %shard_map.77.vec_ref), custom_call_target="tpu_custom_call" | custom-call | tf_op jit(solution)/shard_map/pallas_call | solution.py:289

commit v4 on v3

--- a/solution.py
+++ b/solution.py
@@ -10,6 +10,8 @@
 MESH = pl.DeviceIdType.MESH
 F32 = jnp.float32
 BF16 = jnp.bfloat16
+WIDE = 4
+FAR = 1e30
 CORES = 2
 
 
@@ -18,13 +20,13 @@
 
 
 def kernel(cfg, q_hbm, d_hbm, w_hbm, qm_hbm, dm_hbm, temp_hbm, out_ref,
-           qbuf, dbuf, wbuf, qmbuf, dmbuf, dm8, tbuf, qt_all, p_buf, mcol, s_all,
+           qbuf, dbuf, wbuf, qmbuf, dmbuf, dm8, tbuf, qt_all, p_buf, skip, pick, s_all,
            insem, dsem, qrecv, frecv, sems):
     ny, nx, nq, qlen, ndoc, dlen, rows, depth = cfg
     nchip = ny * nx
     ndev = nchip * CORES
     pass_at = 3
-    wide = 4
+    wide = WIDE
     proj = w_hbm.shape[1]
     lanes = nq * qlen
     na, nb = ny, nx
@@ -109,7 +111,7 @@
     qt_all[mine] = jnp.dot(qn, perm, preferred_element_type=F32).astype(BF16)
 
     copies[3].wait()
-    dm8[...] = jnp.zeros_like(dm8)
+    dm8[...] = jnp.ones_like(dm8)
     dm8[0:ndoc, :] = dmbuf[...].astype(F32)
 
     pl.semaphore_wait(barrier, na + nb - 1)
@@ -146,18 +148,11 @@
 
     for j in range(depth + 1, ndoc):
         doc_copy(j).start()
-    mt = dm8[...].T
-
-    def fill(j):
-        part = pl.ds(j * dlen, dlen)
-        row = dm8[j:j + 1, :]
-        pos = lax.broadcasted_iota(jnp.int32, (1, dlen), 1).astype(F32)
-        first = jnp.min(jnp.where(row > 0, pos, float(dlen)), axis=-1, keepdims=True)
-        pick = jnp.where(pos == first, 1.0, 0.0).astype(BF16)
-        pj = p_buf[part, :]
-        token = jnp.dot(pick, pj, preferred_element_type=F32).astype(BF16)
-        m = mcol[part, :]
-        p_buf[part, :] = pj * m + token * (1 - m)
+    gone = jnp.concatenate([(dm8[...] - 1.0) * FAR, jnp.zeros((proj - 8, dlen), F32)], axis=0)
+    skip[...] = gone.T.astype(BF16)
+    erow = lax.broadcasted_iota(jnp.int32, pick.shape[1:], 0)
+    for j in range(ndoc):
+        pick[j] = jnp.where(erow == j, 1.0, 0.0).astype(BF16)
 
     for j in range(ndoc):
         doc_copy(j).wait()
@@ -166,9 +161,6 @@
         for c in range(dlen // rows):
             part = pl.ds(j * dlen + c * rows, rows)
             p_buf[part, :] = project(dbuf[part, :]).astype(BF16)
-        mcol[pl.ds(j * dlen, dlen), :] = jnp.broadcast_to(mt[:, j:j + 1], (dlen, proj)).astype(BF16)
-        if j > 0:
-            fill(j - 1)
 
     lane = lax.broadcasted_iota(jnp.int32, (8, lanes), 1)
     width = wide * lanes
@@ -198,21 +190,28 @@
         for _, ready in queue[g:g + wide]:
             if ready is not None:
                 ready()
-        if g == 0:
-            fill(ndoc - 1)
         here = [block(*where) for where, _ in queue[g:g + wide]]
         rhs = jnp.concatenate([qt_all[slot] for slot, _ in here], axis=1)
         best = jnp.zeros((8, width), F32)
         for j in range(ndoc):
-            s = jnp.dot(p_buf[pl.ds(j * dlen, dlen), :], rhs, preferred_element_type=F32)
+            s = jnp.dot(jnp.concatenate([p_buf[pl.ds(j * dlen, dlen), :], skip[...]], axis=1),
+                        jnp.concatenate([rhs, pick[j]], axis=0), preferred_element_type=F32)
             s = jnp.max(s.reshape(dlen // 8, 8, width), axis=0)
             best = jnp.where(wsub == j, jnp.max(s, axis=0, keepdims=True), best)
             if j == 0:
                 for item in pending:
                     s_acc = tail(s_acc, *item)
         pending = [(best, [i for _, i in here])]
-    for item in pending:
-        s_acc = tail(s_acc, *item)
+    (best, ids), = pending
+    hi = best.astype(BF16)
+    mid = (best - hi.astype(F32)).astype(BF16)
+    lo = (best - hi.astype(F32) - mid.astype(F32)).astype(BF16)
+    gu = lax.broadcasted_iota(jnp.int32, (lanes, lanes), 0)
+    gl = lax.broadcasted_iota(jnp.int32, (lanes, lanes), 1)
+    same = gu % nq == gl % nq
+    into = jnp.concatenate([jnp.where(same & (gl // nq == i), 1.0, 0.0).astype(BF16) for i in ids], axis=0)
+    parts = jnp.dot(jnp.concatenate([hi, mid, lo], axis=0), into, preferred_element_type=F32)
+    s_acc = s_acc + (parts[:8] + parts[8:16] + parts[16:24])
     copies[4].wait()
     s_all[me] = s_acc[:ndoc, :] / tbuf[0]
 
@@ -278,7 +277,8 @@
                 pltpu.SMEM((1,), F32),
                 pltpu.VMEM((ndev, proj, nq * qlen), BF16),
                 pltpu.VMEM((ndoc * dlen, proj), BF16),
-                pltpu.VMEM((ndoc * dlen, proj), BF16),
+                pltpu.VMEM((dlen, proj), BF16),
+                pltpu.VMEM((ndoc, proj, WIDE * nq * qlen), BF16),
                 pltpu.VMEM((ndev, ndoc, ndev * nq), F32),
                 dma((5,)), dma((ndoc,)), dma((2,)), dma((3,)), dma((4,)),
             ],

time: 27.3 us -> 26.8 us (0.982)
  Pallas kernels: 25.9 us -> 25.4 us
    pallas_call x1, Pallas kernels: 25.4 us -> 24.9 us  [local_step(): pl.pallas_call(functools.partial(kernel, cfg), out_shape=pltpu.VMEM((8, n...]
where the time goes in v4:
time: 26.8 us; the launch traced here: 26.7 us
  Pallas kernels  25.4 us (95%)
  between operations  1.29 us (5%)
    pallas_call x1, Pallas kernels, local_step(): pl.pallas_call(functools.partial(kernel, cfg), out_shape=pltpu.VMEM((8, n...  24.9 us

profile of v4, /device:TPU:97, one launch (start us, length us, event | category | flops | bytes accessed | tf_op | source)
XLA Modules:
  0.0 26.7 jit_solution(8918601090118757208)
XLA Ops:
  1.3 24.9 %shard_map.77.vec_ref = f32[8,128]{1,0:T(8,128)S(1)} custom-call(bf16[128,2048]{1,0:T(8,128)(2,1)} %bitcast.5, bf16[3072,2048]{1,0:T(8,128)(2,1)} %bitcast.4, bf16[2048,128]{1,0:T(8,128)(2,1)} %w_hbm.1, s32[4,32]{1,0:T(4,128)} %qm_hbm.1, s32[4,768]{1,0:T(4,128)} %dm_hbm.1, f32[1]{0:T(128)} %bitcast.3.temp_hbm), custom_call_target="tpu_custom_call" | custom-call | tf_op jit(solution)/shard_map/pallas_call | solution.py:265
  26.2 0.5 %shard_map.78 = (f32[4]{0:T(128)}, f32[1]{0:T(128)}) custom-call(f32[8,128]{1,0:T(8,128)S(1)} %shard_map.77.vec_ref), custom_call_target="tpu_custom_call" | custom-call | tf_op jit(solution)/shard_map/pallas_call | solution.py:289

commit v5 on v4

--- a/solution.py
+++ b/solution.py
@@ -60,13 +60,6 @@
     def wait_bytes(buf, n, sem):
         pltpu.make_async_copy(buf.at[pl.ds(0, n)], buf.at[pl.ds(0, n)], sem).wait()
 
-    barrier = pltpu.get_barrier_semaphore()
-    ring1 = {o: plane_dev(a, step(b, o, nb)) for o in offsets(nb)[::-1]}
-    ring2 = {o: plane_dev(step(a, o, na), b) for o in offsets(na)[::-1]}
-    partner = dev(y, x, other)
-    for d in [*ring2.values(), *ring1.values(), partner]:
-        pl.semaphore_signal(barrier, inc=1, device_id=d, device_id_type=MESH)
-
     copies = [
         pltpu.make_async_copy(q_hbm, qbuf, insem.at[0]),
         pltpu.make_async_copy(w_hbm, wbuf, insem.at[1]),
@@ -83,6 +76,13 @@
 
     for j in range(depth):
         doc_copy(j).start()
+
+    barrier = pltpu.get_barrier_semaphore()
+    ring1 = {o: plane_dev(a, step(b, o, nb)) for o in offsets(nb)[::-1]}
+    ring2 = {o: plane_dev(step(a, o, na), b) for o in offsets(na)[::-1]}
+    partner = dev(y, x, other)
+    for d in [*ring2.values(), *ring1.values(), partner]:
+        pl.semaphore_signal(barrier, inc=1, device_id=d, device_id_type=MESH)
 
     copies[2].wait()
     tok_r = lax.broadcasted_iota(jnp.int32, (qlen, lanes), 0)
@@ -126,8 +126,7 @@
     rest = [(i, j) for i in near for j in offsets(nb)] + [(i, j) for i in far for j in offsets(nb)]
 
     def pass_cross():
-        wait_bytes(qt_all, len(cross1) + len(cross2), qrecv.at[0])
-        wait_bytes(qt_all, 1, frecv.at[0])
+        wait_bytes(qt_all, len(cross1) + len(cross2) + 1, qrecv.at[0])
         for i, j in cross1:
             for o in near:
                 send(block(0, i, j)[0], ring2[o], sems.at[0], qrecv.at[1])
@@ -135,16 +134,16 @@
             for o in offsets(nb):
                 send(block(0, i, 0)[0], ring1[o], sems.at[0], qrecv.at[1])
         for i, j in cross1 + cross2:
-            send(block(0, i, j)[0], partner, sems.at[1], frecv.at[1])
+            send(block(0, i, j)[0], partner, sems.at[0], frecv.at[0])
 
     def pass_rest():
         wait_bytes(qt_all, len(rest), qrecv.at[1])
         for i, j in rest:
-            send(block(0, i, j)[0], partner, sems.at[1], frecv.at[2])
+            send(block(0, i, j)[0], partner, sems.at[0], frecv.at[1])
 
     for d in [*ring2.values(), *ring1.values()]:
         send(mine, d, sems.at[0], qrecv.at[0])
-    send(mine, partner, sems.at[1], frecv.at[0])
+    send(mine, partner, sems.at[0], qrecv.at[0])
 
     for j in range(depth + 1, ndoc):
         doc_copy(j).start()
@@ -178,9 +177,9 @@
 
     arrivals = [
         ([(0, 0, 0)] + [(0, *o) for o in cross1] + [(1, 0, 0)] + [(0, *o) for o in cross2], None),
-        ([(1, *o) for o in cross1 + cross2], lambda: wait_bytes(qt_all, len(cross1) + len(cross2), frecv.at[1])),
+        ([(1, *o) for o in cross1 + cross2], lambda: wait_bytes(qt_all, len(cross1) + len(cross2), frecv.at[0])),
         ([(0, *o) for o in rest], pass_rest),
-        ([(1, *o) for o in rest], lambda: wait_bytes(qt_all, len(rest), frecv.at[2])),
+        ([(1, *o) for o in rest], lambda: wait_bytes(qt_all, len(rest), frecv.at[1])),
     ]
     queue = [(where, ready if n == 0 else None) for blocks, ready in arrivals for n, where in enumerate(blocks)]
 
@@ -220,11 +219,10 @@
     for oy, ox, c in peers:
         pltpu.make_async_remote_copy(
             src_ref=s_all.at[me], dst_ref=s_all.at[me],
-            send_sem=sems.at[2], recv_sem=sems.at[3],
+            send_sem=sems.at[1], recv_sem=sems.at[2],
             device_id=dev(step(y, oy, ny), step(x, ox, nx), step(core, c, CORES)), device_id_type=MESH).start()
-    wait_bytes(qt_all, nchip - 1, sems.at[0])
-    wait_bytes(qt_all, nchip, sems.at[1])
-    wait_bytes(s_all, ndev - 1, sems.at[3])
+    wait_bytes(qt_all, ndev - 1, sems.at[0])
+    wait_bytes(s_all, ndev - 1, sems.at[2])
 
     logits = s_all[...]
     top = jnp.max(jnp.max(logits, axis=0), axis=0, keepdims=True)
@@ -239,7 +237,7 @@
     mean = jnp.sum(losses, axis=1, keepdims=True) / nrow
     out_ref[...] = jnp.where(lax.broadcasted_iota(jnp.int32, home.shape, 0) == 0, home, mean)
 
-    wait_bytes(s_all, ndev - 1, sems.at[2])
+    wait_bytes(s_all, ndev - 1, sems.at[1])
 
 
 def finish(vec_ref, loss_ref, mean_ref):
@@ -280,7 +278,7 @@
                 pltpu.VMEM((dlen, proj), BF16),
                 pltpu.VMEM((ndoc, proj, WIDE * nq * qlen), BF16),
                 pltpu.VMEM((ndev, ndoc, ndev * nq), F32),
-                dma((5,)), dma((ndoc,)), dma((2,)), dma((3,)), dma((4,)),
+                dma((5,)), dma((ndoc,)), dma((2,)), dma((2,)), dma((3,)),
             ],
             compiler_params=pltpu.CompilerParams(
                 collective_id=0, has_side_effects=True, vmem_limit_bytes=60 * 1024 * 1024),

time: 26.8 us -> 26.6 us (level)
  no operation moved by 1% of the time
where the time goes in v5:
time: 26.6 us; the launch traced here: 26.5 us
  Pallas kernels  25.2 us (95%)
  between operations  1.29 us (5%)
    pallas_call x1, Pallas kernels, local_step(): pl.pallas_call(functools.partial(kernel, cfg), out_shape=pltpu.VMEM((8, n...  24.7 us

profile of v5, /device:TPU:97, one launch (start us, length us, event | category | flops | bytes accessed | tf_op | source)
XLA Modules:
  0.0 26.5 jit_solution(4434139626945543170)
XLA Ops:
  1.3 24.7 %shard_map.77.vec_ref = f32[8,128]{1,0:T(8,128)S(1)} custom-call(bf16[128,2048]{1,0:T(8,128)(2,1)} %bitcast.5, bf16[3072,2048]{1,0:T(8,128)(2,1)} %bitcast.4, bf16[2048,128]{1,0:T(8,128)(2,1)} %w_hbm.1, s32[4,32]{1,0:T(4,128)} %qm_hbm.1, s32[4,768]{1,0:T(4,128)} %dm_hbm.1, f32[1]{0:T(128)} %bitcast.3.temp_hbm), custom_call_target="tpu_custom_call" | custom-call | tf_op jit(solution)/shard_map/pallas_call | solution.py:263
  26.0 0.5 %shard_map.78 = (f32[4]{0:T(128)}, f32[1]{0:T(128)}) custom-call(f32[8,128]{1,0:T(8,128)S(1)} %shard_map.77.vec_ref), custom_call_target="tpu_custom_call" | custom-call | tf_op jit(solution)/shard_map/pallas_call | solution.py:287

commit v6 on v5

--- a/solution.py
+++ b/solution.py
@@ -215,7 +215,7 @@
     s_all[me] = s_acc[:ndoc, :] / tbuf[0]
 
     peers = [(oy, ox, c) for oy in range(ny) for ox in range(nx) for c in range(CORES)][1:]
-    peers.sort(key=lambda p: -min(p[0], ny - p[0]) - min(p[1], nx - p[1]))
+    peers.sort(key=lambda p: {3: 0, 4: 1, 2: 2, 1: 3, 0: 4}[min(p[0], ny - p[0]) + min(p[1], nx - p[1])])
     for oy, ox, c in peers:
         pltpu.make_async_remote_copy(
             src_ref=s_all.at[me], dst_ref=s_all.at[me],

time: 26.6 us -> 26.6 us (level)
  no operation moved by 1% of the time
where the time goes in v6:
time: 26.6 us; the launch traced here: 26.5 us
  Pallas kernels  25.2 us (95%)
  between operations  1.29 us (5%)
    pallas_call x1, Pallas kernels, local_step(): pl.pallas_call(functools.partial(kernel, cfg), out_shape=pltpu.VMEM((8, n...  24.7 us

profile of v6, /device:TPU:97, one launch (start us, length us, event | category | flops | bytes accessed | tf_op | source)
XLA Modules:
  0.0 26.5 jit_solution(17773631160361606554)
XLA Ops:
  1.3 24.7 %shard_map.77.vec_ref = f32[8,128]{1,0:T(8,128)S(1)} custom-call(bf16[128,2048]{1,0:T(8,128)(2,1)} %bitcast.5, bf16[3072,2048]{1,0:T(8,128)(2,1)} %bitcast.4, bf16[2048,128]{1,0:T(8,128)(2,1)} %w_hbm.1, s32[4,32]{1,0:T(4,128)} %qm_hbm.1, s32[4,768]{1,0:T(4,128)} %dm_hbm.1, f32[1]{0:T(128)} %bitcast.3.temp_hbm), custom_call_target="tpu_custom_call" | custom-call | tf_op jit(solution)/shard_map/pallas_call | solution.py:263
  26.0 0.5 %shard_map.78 = (f32[4]{0:T(128)}, f32[1]{0:T(128)}) custom-call(f32[8,128]{1,0:T(8,128)S(1)} %shard_map.77.vec_ref), custom_call_target="tpu_custom_call" | custom-call | tf_op jit(solution)/shard_map/pallas_call | solution.py:287
